TPU v7x, 32 devices: a whole 2x2x4 slice. The times are simulated.
32 devices in a mesh: shard: 4 (over y, x), tp: 8 (over z, core).
Axes of the slice: x: 2, y: 2, z: 4, core: 2. Of those that a mesh axis runs over, the one named last changes fastest.
Arguments:
- w_gate: float32 [5120, 17408], P('shard', 'tp'), may hold values from -0.125 to 0.125
- first_gate: float32 [5120, 17408], P('shard', 'tp'), may hold values from -0.078125 to 0.078125
- second_gate: float32 [5120, 17408], P('shard', 'tp'), may hold values from -0.078125 to 0.078125
- w_up: float32 [5120, 17408], P('shard', 'tp'), may hold values from -0.125 to 0.125
- first_up: float32 [5120, 17408], P('shard', 'tp'), may hold values from -0.078125 to 0.078125
- second_up: float32 [5120, 17408], P('shard', 'tp'), may hold values from -0.078125 to 0.078125
- norm_gain: float32 [5120], P('shard'), may hold values from 0.25 to 1.75
Outputs:
- serving_gate: bfloat16 [5120, 17408], P(None, 'tp')
- serving_up: bfloat16 [5120, 17408], P(None, 'tp')
- column_gate: float32 [17408], P('tp')
- column_up: float32 [17408], P('tp')
All inputs are finite; a program needn't handle non-finite values.
Results may differ from a plain program's by a relative error of at most 0.001.
Values may be sent and summed in bfloat16 or wider, within the bound.
A program may use at most 256 MiB of HBM per device.

v0:
```python
import jax
import jax.numpy as jnp
from jax import lax
from jax.sharding import PartitionSpec as P

learn_rate = 0.2
hold_rate = 0.8


def per_device(w_gate, first_gate, second_gate, w_up, first_up, second_up, norm_gain):
    hold_gate = hold_rate * first_gate + second_gate
    whole_gate = w_gate - learn_rate * hold_gate
    hold_up = hold_rate * first_up + second_up
    whole_up = w_up - learn_rate * hold_up
    whole_gained_gate = whole_gate * norm_gain[:, None]
    whole_gained_up = whole_up * norm_gain[:, None]
    total_gate, total_up = lax.psum(
        (
            jnp.sum(whole_gained_gate * whole_gained_gate, axis=0),
            jnp.sum(whole_gained_up * whole_gained_up, axis=0),
        ),
        "shard",
    )
    column_gate = jnp.sqrt(total_gate)
    column_up = jnp.sqrt(total_up)
    narrow_gate, narrow_up = (
        (whole_gained_gate / column_gate).astype(jnp.bfloat16),
        (whole_gained_up / column_up).astype(jnp.bfloat16),
    )
    serving_gate, serving_up = (
        lax.all_gather(narrow_gate, "shard", axis=0, tiled=True),
        lax.all_gather(narrow_up, "shard", axis=0, tiled=True),
    )
    return (serving_gate, serving_up, column_gate, column_up)


def solution(mesh):
    return jax.shard_map(
        per_device,
        mesh=mesh,
        in_specs=(
            P("shard", "tp"),
            P("shard", "tp"),
            P("shard", "tp"),
            P("shard", "tp"),
            P("shard", "tp"),
            P("shard", "tp"),
            P("shard"),
        ),
        out_specs=(P(None, "tp"), P(None, "tp"), P("tp"), P("tp")),
        check_vma=False,
    )
```

profile of v0, /device:TPU:0, one launch (start us, length us, event | category | flops | bytes accessed | tf_op | source)
XLA Modules:
  0.0 509.6 jit_solution(11338734941351537745)
XLA Ops:
  7.2 0.0 all-gather.3.cloned.1.call-start
  7.2 30.6 %multiply_reduce_fusion = (f32[2176]{0:T(1024)S(1)}, f32[1280,2176]{1,0:T(8,128)}, f32[2176]{0:T(1024)S(1)}, f32[1280,2176]{1,0:T(8,128)}) fusion(f32[1280]{0:T(1024)} %param.13, f32[1280,2176]{1,0:T(8,128)} %param.10, f32[1280,2176]{1,0:T(8,128)} %param.12, f32[1280,2176]{1,0:T(8,128)} %param.11, f32[1280,2176]{1,0:T(8,128)} %param.7, ...), kind=kLoop, calls=%fused_computation.1 | loop fusion | flops 38989568 | bytes 89151488 | tf_op jit(solution)/shard_map/reduce_sum | solution.py:20
  37.9 17.7 %all-reduce = (f32[2176]{0:T(1024)S(1)}, f32[2176]{0:T(1024)S(1)}) all-reduce(f32[2176]{0:T(1024)S(1)} %get-tuple-element.10, f32[2176]{0:T(1024)S(1)} %get-tuple-element.6), channel_id=1, replica_groups=mesh['shard'=4,'tp'=8] {'shard'}, use_global_device_ids=true, to_apply=%region_1.0 | all-reduce | flops 4352 | bytes 34816 | tf_op jit(solution)/shard_map/psum | solution.py:17
  55.6 0.0 copy-start.1
  55.6 7.4 %divide_convert_fusion.1 = bf16[1280,2176]{1,0:T(8,128)(2,1)} fusion(f32[1280,2176]{1,0:T(8,128)} %get-tuple-element.11, f32[2176]{0:T(1024)S(1)} %sqrt.6), kind=kLoop, calls=%fused_computation.3 | loop fusion | flops 5570560 | bytes 16720384 | tf_op jit(solution)/shard_map/convert_element_type | solution.py:27
  62.9 0.0 all-gather.3.cloned.1.call-update
  63.0 0.0 copy-done.1
  63.0 0.0 all-gather.5.cloned.1.call-start
  63.0 0.0 copy-start.2
  63.0 8.6 %divide_convert_fusion = bf16[1280,2176]{1,0:T(8,128)(2,1)} fusion(f32[1280,2176]{1,0:T(8,128)} %get-tuple-element.7, f32[2176]{0:T(1024)S(1)} %sqrt.7), kind=kLoop, calls=%fused_computation | loop fusion | flops 5570560 | bytes 16720384 | tf_op jit(solution)/shard_map/convert_element_type | solution.py:28
  71.7 0.0 all-gather.5.cloned.1.call-update
  71.7 0.0 copy-done.2
  71.7 194.7 %all-gather.3.cloned.1.call-done = bf16[5120,2176]{1,0:T(8,128)(2,1)} async-done(((bf16[1280,2176]{1,0:T(8,128)(2,1)}), bf16[5120,2176]{1,0:T(8,128)(2,1)}) %all-gather.3.cloned.1.call-update) | async-done | bytes 22282256 | tf_op jit(solution)/shard_map/all_gather | solution.py:31
  266.4 206.3 %all-gather.5.cloned.1.call-done = bf16[5120,2176]{1,0:T(8,128)(2,1)} async-done(((bf16[1280,2176]{1,0:T(8,128)(2,1)}), bf16[5120,2176]{1,0:T(8,128)(2,1)}) %all-gather.5.cloned.1.call-update) | async-done | bytes 22282256 | tf_op jit(solution)/shard_map/all_gather | solution.py:32
  472.7 0.0 copy-start
  472.7 20.5 %copy.13 = bf16[5120,2176]{1,0:T(8,128)(2,1)} copy(bf16[5120,2176]{1,0:T(8,128)(2,1)} %all-gather.3.cloned.1.call-done) | data formatting | bytes 44564480
  493.2 1.5 copy-done
  494.8 8.0 %copy.14 = bf16[5120,2176]{1,0:T(8,128)(2,1)} copy(bf16[5120,2176]{1,0:T(8,128)(2,1)S(1)} %copy-done) | data formatting | bytes 44564480
  (2 shorter events, 0.0 us)
Async XLA Ops:
  7.2 259.2 %all-gather.3.cloned.1.call-start = ((), (), s32[]{:S(2)}) async-start(), calls=%async_computation | async-start | bytes 27852800 | tf_op jit(solution)/shard_map/all_gather | solution.py:31
  55.6 7.4 %copy-start.1 = (f32[2176]{0:T(1024)}, f32[2176]{0:T(1024)S(1)}, u32[]{:S(2)}) copy-start(f32[2176]{0:T(1024)S(1)} %sqrt.6) | copy-start | bytes 26116
  63.0 409.7 %all-gather.5.cloned.1.call-start = ((), (), s32[]{:S(2)}) async-start(), calls=%async_computation.1 | async-start | bytes 27852800 | tf_op jit(solution)/shard_map/all_gather | solution.py:32
  63.0 8.7 %copy-start.2 = (f32[2176]{0:T(1024)}, f32[2176]{0:T(1024)S(1)}, u32[]{:S(2)}) copy-start(f32[2176]{0:T(1024)S(1)} %sqrt.7) | copy-start | bytes 26116
  472.7 22.1 %copy-start = (bf16[5120,2176]{1,0:T(8,128)(2,1)S(1)}, bf16[5120,2176]{1,0:T(8,128)(2,1)}, u32[]{:S(2)}) copy-start(bf16[5120,2176]{1,0:T(8,128)(2,1)} %all-gather.5.cloned.1.call-done) | copy-start | bytes 66846724
Sparse Core Ops, SparseCore 0:
  63.1 203.2 all-gather.2
  268.8 203.8 all-gather.4
where the time goes:
time: 510 us
  waiting for transfers between devices  401 us (79%)
  other arithmetic  46.6 us (9%)
  local copies, waits for them, and re-layouts  30.1 us (6%)
  blocking collectives  17.7 us (3%)
  between operations  14.1 us (3%)
    all_gather x1, waiting for transfers between devices, per_device(): lax.all_gather(narrow_up, 'shard', axis=0, tiled=True)  206 us
    all_gather x1, waiting for transfers between devices, per_device(): lax.all_gather(narrow_gate, 'shard', axis=0, tiled=True)  195 us
    reduce_sum x1, other arithmetic, per_device(): jnp.sum(whole_gained_up * whole_gained_up, axis=0)  30.6 us
    unnamed x8, local copies, waits for them, and re-layouts  30.1 us
    psum x1, blocking collectives, per_device(): lax.psum((jnp.sum(whole_gained_gate * whole_gained_gate, axis=0), jnp.sum...  17.7 us
  transfers between devices with their start and end apart: 2, of which 2 were waited for; matrix products, arithmetic and copies ran while one was open for 2% of the time, Pallas kernels for 0%

commit v1 on v0

--- a/solution.py
+++ b/solution.py
@@ -1,13 +1,21 @@
+import functools
+
 import jax
 import jax.numpy as jnp
 from jax import lax
+from jax.experimental import pallas as pl
+from jax.experimental.pallas import tpu as pltpu
 from jax.sharding import PartitionSpec as P
 
 learn_rate = 0.2
 hold_rate = 0.8
 
-
-def per_device(w_gate, first_gate, second_gate, w_up, first_up, second_up, norm_gain):
+LANES = 128
+STEP = 32
+MESH = pl.DeviceIdType.MESH
+
+
+def plain(w_gate, first_gate, second_gate, w_up, first_up, second_up, norm_gain):
     hold_gate = hold_rate * first_gate + second_gate
     whole_gate = w_gate - learn_rate * hold_gate
     hold_up = hold_rate * first_up + second_up
@@ -23,15 +31,244 @@
     )
     column_gate = jnp.sqrt(total_gate)
     column_up = jnp.sqrt(total_up)
-    narrow_gate, narrow_up = (
-        (whole_gained_gate / column_gate).astype(jnp.bfloat16),
-        (whole_gained_up / column_up).astype(jnp.bfloat16),
-    )
     serving_gate, serving_up = (
-        lax.all_gather(narrow_gate, "shard", axis=0, tiled=True),
-        lax.all_gather(narrow_up, "shard", axis=0, tiled=True),
+        lax.all_gather((whole_gained_gate / column_gate).astype(jnp.bfloat16), "shard", axis=0, tiled=True),
+        lax.all_gather((whole_gained_up / column_up).astype(jnp.bfloat16), "shard", axis=0, tiled=True),
     )
     return (serving_gate, serving_up, column_gate, column_up)
+
+
+def cut(width, starts, most):
+    tiles, sizes = width // LANES, []
+    for size in starts:
+        if tiles > size:
+            sizes.append(size)
+            tiles -= size
+    while tiles > 0:
+        sizes.append(min(most, tiles))
+        tiles -= sizes[-1]
+    chunks, at = [], 0
+    for size in sizes:
+        chunks.append((at * LANES, size * LANES))
+        at += size
+    return chunks
+
+
+def kernel(
+    chunks,
+    rows,
+    width,
+    w_gate,
+    first_gate,
+    second_gate,
+    w_up,
+    first_up,
+    second_up,
+    gain,
+    out_gate,
+    out_up,
+    columns,
+    held,
+    narrow,
+    sums,
+    load_sem,
+    sum_send,
+    sum_recv,
+    own_send,
+    own_recv,
+    pass_send,
+    pass_recv,
+    local_sem,
+):
+    me = lax.axis_index("shard")
+    row, column = me // 2, me % 2
+    beside = row * 2 + (1 - column)
+    above = (1 - row) * 2 + column
+    across = (1 - row) * 2 + (1 - column)
+    sources = ((w_gate, first_gate, second_gate), (w_up, first_up, second_up))
+    outs = (out_gate, out_up)
+    half = rows // 2
+
+    def loads(k):
+        which, first, size = chunks[k]
+        return [
+            pltpu.make_async_copy(
+                ref.at[:, pl.ds(first, size)],
+                held.at[k % 2, i, :, pl.ds(0, size)],
+                load_sem.at[k % 2, i],
+            )
+            for i, ref in enumerate(sources[which])
+        ]
+
+    def send_sums(k):
+        which, first, size = chunks[k]
+        part = sums.at[me, :, pl.ds(which * width + first, size)]
+        return [
+            pltpu.make_async_remote_copy(
+                src_ref=part,
+                dst_ref=part,
+                send_sem=sum_send.at[k, j],
+                recv_sem=sum_recv.at[k, j],
+                device_id={"shard": to},
+                device_id_type=MESH,
+            )
+            for j, to in enumerate((beside, above, across))
+        ]
+
+    def send_own(k):
+        which, first, size = chunks[k]
+        return [
+            pltpu.make_async_remote_copy(
+                src_ref=narrow.at[:, pl.ds(which * width + first, size)],
+                dst_ref=outs[which].at[pl.ds(me * rows, rows), pl.ds(first, size)],
+                send_sem=own_send.at[k, j],
+                recv_sem=own_recv.at[k, j],
+                device_id={"shard": to},
+                device_id_type=MESH,
+            )
+            for j, to in enumerate((beside, above))
+        ]
+
+    def keep_own(k):
+        which, first, size = chunks[k]
+        return pltpu.make_async_copy(
+            narrow.at[:, pl.ds(which * width + first, size)],
+            outs[which].at[pl.ds(me * rows, rows), pl.ds(first, size)],
+            local_sem.at[k],
+        )
+
+    def send_on(k):
+        which, first, size = chunks[k]
+        copies = []
+        for j, (origin, to) in enumerate(((above, beside), (beside, above))):
+            part = outs[which].at[pl.ds(origin * rows + j * half, half), pl.ds(first, size)]
+            copies.append(
+                pltpu.make_async_remote_copy(
+                    src_ref=part,
+                    dst_ref=part,
+                    send_sem=pass_send.at[k, j],
+                    recv_sem=pass_recv.at[k, j],
+                    device_id={"shard": to},
+                    device_id_type=MESH,
+                )
+            )
+        return copies
+
+    for k in range(min(2, len(chunks))):
+        for copy in loads(k):
+            copy.start()
+    barrier = pltpu.get_barrier_semaphore()
+    for peer in (beside, above, across):
+        pl.semaphore_signal(barrier, inc=1, device_id={"shard": peer}, device_id_type=MESH)
+
+    for k, (which, first, size) in enumerate(chunks):
+        slot, tiles = k % 2, size // LANES
+        for copy in loads(k):
+            copy.wait()
+
+        def add_up(step, totals):
+            here = pl.ds(pl.multiple_of(step * STEP, STEP), STEP)
+            scale = gain[here, :]
+            new = []
+            for t in range(tiles):
+                lanes = pl.ds(t * LANES, LANES)
+                hold = hold_rate * held[slot, 1, here, lanes] + held[slot, 2, here, lanes]
+                value = (held[slot, 0, here, lanes] - learn_rate * hold) * scale
+                held[slot, 0, here, lanes] = value
+                new.append(totals[t] + jnp.sum((value * value).reshape(STEP // 8, 8, LANES), axis=0))
+            return tuple(new)
+
+        totals = lax.fori_loop(
+            0, rows // STEP, add_up, tuple(jnp.zeros((8, LANES), jnp.float32) for _ in range(tiles))
+        )
+        for t in range(tiles):
+            sums[me, :, pl.ds(which * width + first + t * LANES, LANES)] = totals[t]
+        if k == 0:
+            pl.semaphore_wait(barrier, 3)
+        exchange = send_sums(k)
+        for copy in exchange:
+            copy.start()
+        for copy in exchange:
+            copy.wait_recv()
+        place = pl.ds(which * width + first, size)
+        total = (sums[0, :, place] + sums[1, :, place]) + (sums[2, :, place] + sums[3, :, place])
+        scale_of = jnp.sqrt(jnp.sum(total, axis=0, keepdims=True))
+        columns[which : which + 1, pl.ds(first, size)] = scale_of
+        inverse = 1.0 / scale_of
+
+        def narrow_down(step, carry):
+            here = pl.ds(pl.multiple_of(step * STEP, STEP), STEP)
+            for t in range(tiles):
+                value = held[slot, 0, here, pl.ds(t * LANES, LANES)]
+                factor = inverse[:, t * LANES : (t + 1) * LANES]
+                narrow[here, pl.ds(which * width + first + t * LANES, LANES)] = (value * factor).astype(jnp.bfloat16)
+            return carry
+
+        lax.fori_loop(0, rows // STEP, narrow_down, 0)
+        for copy in send_own(k):
+            copy.start()
+        keep_own(k).start()
+        if k + 2 < len(chunks):
+            for copy in loads(k + 2):
+                copy.start()
+
+    for k in range(len(chunks)):
+        arrived = send_own(k)
+        onward = send_on(k)
+        arrived[1].wait_recv()
+        onward[0].start()
+        arrived[0].wait_recv()
+        onward[1].start()
+
+    for k in range(len(chunks)):
+        for copy in send_sums(k):
+            copy.wait_send()
+        for copy in send_own(k):
+            copy.wait_send()
+        keep_own(k).wait()
+        for copy in send_on(k):
+            copy.wait()
+
+
+def per_device(w_gate, first_gate, second_gate, w_up, first_up, second_up, norm_gain):
+    rows, width = w_gate.shape
+    shards = lax.axis_size("shard")
+    if shards != 4 or width % LANES or rows % (2 * STEP):
+        return plain(w_gate, first_gate, second_gate, w_up, first_up, second_up, norm_gain)
+    chunks = [(0, *chunk) for chunk in cut(width, (1, 2), 4)] + [(1, *chunk) for chunk in cut(width, (), 4)]
+    most = max(size for _, _, size in chunks)
+    count = len(chunks)
+    gain = jnp.broadcast_to(norm_gain[:, None], (rows, LANES))
+    anywhere = pl.BlockSpec(memory_space=pl.ANY)
+    in_vmem = pl.BlockSpec(memory_space=pltpu.VMEM)
+    dma = pltpu.SemaphoreType.DMA
+    serving_gate, serving_up, columns = pl.pallas_call(
+        functools.partial(kernel, chunks, rows, width),
+        out_shape=(
+            jax.ShapeDtypeStruct((shards * rows, width), jnp.bfloat16),
+            jax.ShapeDtypeStruct((shards * rows, width), jnp.bfloat16),
+            jax.ShapeDtypeStruct((2, width), jnp.float32),
+        ),
+        in_specs=[anywhere] * 6 + [in_vmem],
+        out_specs=(anywhere, anywhere, in_vmem),
+        scratch_shapes=[
+            pltpu.VMEM((2, 3, rows, most), jnp.float32),
+            pltpu.VMEM((rows, 2 * width), jnp.bfloat16),
+            pltpu.VMEM((4, 8, 2 * width), jnp.float32),
+            dma((2, 3)),
+            dma((count, 3)),
+            dma((count, 3)),
+            dma((count, 2)),
+            dma((count, 2)),
+            dma((count, 2)),
+            dma((count, 2)),
+            dma((count,)),
+        ],
+        compiler_params=pltpu.CompilerParams(
+            collective_id=0, has_side_effects=True, vmem_limit_bytes=48 * 1024 * 1024
+        ),
+    )(w_gate, first_gate, second_gate, w_up, first_up, second_up, gain)
+    return (serving_gate, serving_up, columns[0], columns[1])
 
 
 def solution(mesh):

time: 510 us -> 408 us (0.80)
  waiting for transfers between devices: 401 us -> 0 us
  Pallas kernels: 0 us -> 375 us
  other arithmetic: 46.6 us -> 0.01 us
  blocking collectives: 17.7 us -> 0 us
  between operations: 14.1 us -> 0.7 us
    all_gather x2 -> x0, waiting for transfers between devices: 401 us -> none  [the longest x1 206 us: per_device(): lax.all_gather(narrow_up, 'shard', axis=0, tiled=True)]
    pallas_call x0 -> x1, Pallas kernels: none -> 375 us  [per_device(): pl.pallas_call(functools.partial(kernel, chunks, rows, width), out_shape=...]
    reduce_sum x1 -> x0, other arithmetic: 30.6 us -> none  [per_device(): jnp.sum(whole_gained_up * whole_gained_up, axis=0)]
    psum x1 -> x0, blocking collectives: 17.7 us -> none  [per_device(): lax.psum((jnp.sum(whole_gained_gate * whole_gained_gate, axis=0), jnp.sum...]
    convert_element_type x2 -> x0, other arithmetic: 16 us -> none  [the longest x1 8.63 us: per_device(): (whole_gained_up / column_up).astype(jnp.bfloat16)]
    unnamed x8 -> x14, local copies, waits for them, and re-layouts: 30.1 us -> 30.7 us
  transfers between devices with their start and end apart: 2 -> 0, of which waited for: 2 -> 0; matrix products, arithmetic and copies ran while one was open for 2% -> 0% of each run, Pallas kernels for 0% -> 0%
where the time goes in v1:
time: 408 us
  Pallas kernels  375 us (92%)
  local copies, waits for them, and re-layouts  32.3 us (8%)
    pallas_call x1, Pallas kernels, per_device(): pl.pallas_call(functools.partial(kernel, chunks, rows, width), out_shape=...  375 us
    unnamed x14, local copies, waits for them, and re-layouts  30.7 us

profile of v1, /device:TPU:0, one launch (start us, length us, event | category | flops | bytes accessed | tf_op | source)
XLA Modules:
  0.0 408.2 jit_solution(8909737863663012365)
XLA Ops:
  0.6 0.9 broadcast_in_dim.2.gain
  1.6 375.2 %shard_map.102 = (bf16[5120,2176]{1,0:T(8,128)(2,1)}, bf16[5120,2176]{1,0:T(8,128)(2,1)}, f32[2,2176]{1,0:T(2,128)S(1)}) custom-call(f32[1280,2176]{1,0:T(8,128)} %w_gate.1, f32[1280,2176]{1,0:T(8,128)} %first_gate.1, f32[1280,2176]{1,0:T(8,128)} %second_gate.1, f32[1280,2176]{1,0:T(8,128)} %w_up.1, f32[1280,2176]{1,0:T(8,128)} %first_up.1, ...), custom_call_target="tpu_custom_call" | custom-call | tf_op jit(solution)/shard_map/pallas_call | solution.py:245
  376.8 0.6 slice_reduce_fusion
  377.5 0.0 slice-start
  377.5 0.0 slice-start.1
  377.5 0.0 slice-start.2
  377.5 0.0 slice-start.3
  377.5 0.0 slice-start.4
  377.5 0.0 slice-start.5
  377.5 22.7 %copy.13 = bf16[5120,2176]{1,0:T(8,128)(2,1)} copy(bf16[5120,2176]{1,0:T(8,128)(2,1)} %get-tuple-element.16) | data formatting | bytes 44564480
  400.2 0.0 slice-done
  400.2 0.0 slice-done.1
  400.2 0.0 slice-done.2
  400.2 0.0 slice-done.3
  400.2 0.0 slice-done.4
  400.3 0.0 slice-done.5
  400.3 8.0 %copy.14 = bf16[5120,2176]{1,0:T(8,128)(2,1)} copy(bf16[5120,2176]{1,0:T(8,128)(2,1)S(1)} %bitcast.1) | data formatting | bytes 44564480
  (1 shorter events, 0.0 us)
Async XLA Ops:
  377.5 22.8 %slice-start = ((s8[22282240]{0:T(1024)(128)(4,1)}), s8[4194304]{0:T(1024)(128)(4,1)S(1)}, s32[]{:S(2)}) async-start(s8[22282240]{0:T(1024)(128)(4,1)} %bitcast), calls=%async_computation | async-start | bytes 8388608
  377.5 22.8 %slice-start.1 = ((s8[22282240]{0:T(1024)(128)(4,1)}), s8[4194304]{0:T(1024)(128)(4,1)S(1)}, s32[]{:S(2)}) async-start(s8[22282240]{0:T(1024)(128)(4,1)} %bitcast), calls=%async_computation.1 | async-start | bytes 8388608
  377.5 22.8 %slice-start.2 = ((s8[22282240]{0:T(1024)(128)(4,1)}), s8[4194304]{0:T(1024)(128)(4,1)S(1)}, s32[]{:S(2)}) async-start(s8[22282240]{0:T(1024)(128)(4,1)} %bitcast), calls=%async_computation.2 | async-start | bytes 8388608
  377.5 22.8 %slice-start.3 = ((s8[22282240]{0:T(1024)(128)(4,1)}), s8[4194304]{0:T(1024)(128)(4,1)S(1)}, s32[]{:S(2)}) async-start(s8[22282240]{0:T(1024)(128)(4,1)} %bitcast), calls=%async_computation.3 | async-start | bytes 8388608
  377.5 22.8 %slice-start.4 = ((s8[22282240]{0:T(1024)(128)(4,1)}), s8[4194304]{0:T(1024)(128)(4,1)S(1)}, s32[]{:S(2)}) async-start(s8[22282240]{0:T(1024)(128)(4,1)} %bitcast), calls=%async_computation.4 | async-start | bytes 8388608
  377.5 22.8 %slice-start.5 = ((s8[22282240]{0:T(1024)(128)(4,1)}), s8[1310720]{0:T(1024)(128)(4,1)S(1)}, s32[]{:S(2)}) async-start(s8[22282240]{0:T(1024)(128)(4,1)} %bitcast), calls=%async_computation.5 | async-start | bytes 2621440
